TPU v7x, 1024 devices: a whole 8x8x8 slice. The times are simulated.
1024 devices in a mesh: comp: 2 (over core), blk: 512 (over y, z, x).
Axes of the slice: x: 8, y: 8, z: 8, core: 2. Of those that a mesh axis runs over, the one named last changes fastest.
Arguments:
- initial: float32 [2, 5, 4096, 2048], P('comp', None, 'blk'), may hold values from -3 to 3
- ice_forcing: float32 [5, 4096, 2048], P(None, 'blk'), may hold values from -2 to 4, as said below
- ocean_current: float32 [2, 4096, 2048], P(None, 'blk'), may hold values from -1 to 1
- ice_cover: int32 [4096, 2048], P('blk'), may hold values from 0 to 1, as said below
- targets: int32 [2, 4096, 2048], P(None, 'blk'), may hold values from 0 to 32767, as said below
- weights: int32 [2, 4096, 2048], P(None, 'blk'), may hold values from 1 to 4
Outputs:
- state_out: float32 [2, 5, 4096, 2048], P('comp', None, 'blk')
- coupled: float32 [2, 3, 4096, 2048], P('comp', None, 'blk')
Inputs may be any that keep to these rules, and one draw needn't show every extreme that they name: `ice_forcing`: channel 0 (mass) lies in 0.5 to 4, channel 1 (strength) and channel 4 (melt rate) in 0.2 to 2, channels 2 and 3 (wind stress) in -2 to 2. `ice_cover`: the share of ice-covered cells differs from strip to strip of 8 rows. `targets`: an entry of an ice cell at row r of its strip names an ocean row of the window no earlier than r.
All inputs are finite; a program needn't handle non-finite values.
Results may differ from a plain program's by a relative error of at most 0.0003.
Values sent between devices are 32-bit elements; how exact they have to be, the bound alone decides.
A program may use at most 128 MiB of HBM per device.

v0:
```python
import jax
import jax.numpy as jnp
from jax import lax
from jax.sharding import PartitionSpec as P

SUBCYCLES = 16


relax_rate = 0.5
ecc_sq = 4.0
delta_floor = 0.1
coriolis = 0.1
drag_coef = 1.0
inertia = 4.0
courant = 0.2
dilution = 0.5
weight_norm = 4.0
level_speed = (1.0, 0.8, 0.6, 0.45, 0.3)


def extended_2(block, sides, width):
    for axis, dim in sides:
        count = lax.axis_size(axis)
        forward = [(i, i + 1) for i in range(count - 1)]
        backward = [(target, source) for source, target in forward]
        low = lax.ppermute(
            lax.slice_in_dim(block, block.shape[dim] - width, None, axis=dim), axis, forward
        )
        high = lax.ppermute(lax.slice_in_dim(block, 0, width, axis=dim), axis, backward)
        block = jnp.concatenate([low, block, high], axis=dim)
    return block


def shifted(value, axis, steps):
    count = lax.axis_size(axis)
    first, last = (max(0, -steps), min(count, count - steps))
    return lax.ppermute(value, axis, [(source, source + steps) for source in range(first, last)])


def from_behind(value, axis, steps):
    count = lax.axis_size(axis)
    pairs = [(source, (source + steps) % count) for source in range(count)]
    return lax.ppermute(value, axis, pairs)


def along_rows(field):
    return 0.5 * (field[..., 2:, :] - field[..., :-2, :])


def across(field):
    padded = jnp.pad(field, [(0, 0)] * (field.ndim - 1) + [(1, 1)])
    return 0.5 * (padded[..., 2:] - padded[..., :-2])


def ice_step(fields, forcing, current, covered):
    vel_x = fields[0]
    vel_y = fields[1]
    strain_d = along_rows(vel_x) + across(vel_y[1:-1])
    strain_t = along_rows(vel_x) - across(vel_y[1:-1])
    strain_s = across(vel_x[1:-1]) + along_rows(vel_y)
    delta = jnp.sqrt(
        strain_d * strain_d
        + (strain_t * strain_t + strain_s * strain_s) / ecc_sq
        + delta_floor * delta_floor
    )
    press = forcing[1, 1:-1] * covered[1:-1]
    sig_one = (fields[2, 1:-1] + relax_rate * press * (strain_d / delta - 1.0)) / (1.0 + relax_rate)
    sig_two = (fields[3, 1:-1] + relax_rate * press * strain_t / (ecc_sq * delta)) / (
        1.0 + relax_rate
    )
    sig_shear = (fields[4, 1:-1] + relax_rate * press * strain_s / (2.0 * ecc_sq * delta)) / (
        1.0 + relax_rate
    )
    sig_xx = 0.5 * (sig_one + sig_two)
    sig_yy = 0.5 * (sig_one - sig_two)
    force_x = along_rows(sig_xx) + across(sig_shear[1:-1])
    force_y = along_rows(sig_shear) + across(sig_yy[1:-1])
    beta = inertia * forcing[0, 2:-2]
    old_x = vel_x[2:-2]
    old_y = vel_y[2:-2]
    denom = beta + drag_coef
    new_x = (
        covered[2:-2]
        * (
            beta * old_x
            + coriolis * beta * old_y
            + force_x
            + forcing[2, 2:-2]
            + drag_coef * current[0, 2:-2]
        )
        / denom
    )
    new_y = (
        covered[2:-2]
        * (
            beta * old_y
            - coriolis * beta * old_x
            + force_y
            + forcing[3, 2:-2]
            + drag_coef * current[1, 2:-2]
        )
        / denom
    )
    return jnp.stack([new_x, new_y, sig_one[1:-1], sig_two[1:-1], sig_shear[1:-1]])


def ocean_step(tracer, current):
    speed = jnp.asarray(level_speed, jnp.float32)[:, None, None]
    centre = tracer[:, 2:-2]
    below = centre - tracer[:, 1:-3]
    above = tracer[:, 3:-1] - centre
    padded = jnp.pad(centre, ((0, 0), (0, 0), (1, 1)))
    left_diff = centre - padded[:, :, :-2]
    right_diff = padded[:, :, 2:] - centre
    speed_x = speed * current[0, 2:-2][None]
    speed_y = speed * current[1, 2:-2][None]
    change = (
        jnp.maximum(speed_x, 0.0) * below
        + jnp.minimum(speed_x, 0.0) * above
        + jnp.maximum(speed_y, 0.0) * left_diff
        + jnp.minimum(speed_y, 0.0) * right_diff
    )
    return centre - courant * change


def coupling_terms(fields, forcing, current, covered):
    stress_x = covered * drag_coef * (fields[0] - current[0])
    stress_y = covered * drag_coef * (fields[1] - current[1])
    fresh = forcing[4] * covered * jnp.sqrt(1.0 + fields[0] * fields[0] + fields[1] * fields[1])
    return jnp.stack([stress_x, stress_y, fresh])


def remap_window(values, targets, weights):
    scaled = weights.astype(jnp.float32) / weight_norm
    window_size = 2 * values.shape[1] * values.shape[2]
    flat_targets = targets.reshape(-1)

    def spread(single):
        return jax.ops.segment_sum(
            (single[None] * scaled).reshape(-1), flat_targets, num_segments=window_size
        )

    return jax.vmap(spread)(values)


def body(initial, ice_forcing, ocean_current, ice_cover, targets, weights):
    depth = 2
    width = 2 * depth
    is_ice = lax.axis_index("comp") == 0
    row_count = initial.shape[2]
    col_count = initial.shape[3]
    covered = ice_cover.astype(jnp.float32)
    statics = jnp.concatenate([ice_forcing, ocean_current, covered[None]], axis=0)
    static_ext = extended_2(statics, (("blk", 1),), width)
    forcing_ext = static_ext[:5]
    current_ext = static_ext[5:7]
    cover_ext = static_ext[7]
    empty_total = jnp.zeros((3, row_count, col_count), jnp.float32)

    def ice_turns(extended):
        fields = extended
        total = empty_total
        for turn in range(depth):
            lower = 2 * turn
            upper = row_count + 2 * width - 2 * turn
            fields = ice_step(
                fields,
                forcing_ext[:, lower:upper],
                current_ext[:, lower:upper],
                cover_ext[lower:upper],
            )
            own_start = width - 2 * (turn + 1)
            own_fields = fields[:, own_start : own_start + row_count]
            total = total + coupling_terms(own_fields, ice_forcing, ocean_current, covered)
        return (fields, total)

    def ocean_turns(extended):
        fields = extended
        for turn in range(depth):
            lower = 2 * turn
            upper = row_count + 2 * width - 2 * turn
            fields = ocean_step(fields, current_ext[:, lower:upper])
        return (fields, empty_total)

    def advance(step_index, carry):
        fields, total = carry
        extended = extended_2(fields, (("blk", 1),), width)
        fields, extra = lax.cond(is_ice, ice_turns, ocean_turns, extended)
        return (fields, total + extra)

    fields, total = lax.fori_loop(0, SUBCYCLES // depth, advance, (initial[0], empty_total))
    average = total / SUBCYCLES
    empty_window = jnp.zeros((3, 2 * row_count * col_count), jnp.float32)

    def window_sums(values):
        return remap_window(values, targets, weights)

    def no_window(values):
        return empty_window

    partial_sums = lax.cond(is_ice, window_sums, no_window, average)
    window = shifted(partial_sums, "comp", 1)
    half_size = row_count * col_count
    from_before = from_behind(window[:, half_size:], "blk", 1)
    flux = (window[:, :half_size] + from_before).reshape(3, row_count, col_count)

    def ice_result(fields, flux):
        return (fields, average)

    def ocean_result(fields, flux):
        salinity = jnp.concatenate([fields[:1] - dilution * flux[2][None], fields[1:]], axis=0)
        return (salinity, flux)

    final_state, coupled = lax.cond(is_ice, ice_result, ocean_result, fields, flux)
    return (final_state[None], coupled[None])


def solution(mesh):
    placed = (
        P("comp", None, "blk", None),
        P(None, "blk", None),
        P(None, "blk", None),
        P("blk", None),
        P(None, "blk", None),
        P(None, "blk", None),
    )
    return jax.shard_map(
        body,
        mesh=mesh,
        in_specs=placed,
        out_specs=(P("comp", None, "blk", None), P("comp", None, "blk", None)),
        check_vma=False,
    )
```

profile of v0, /device:TPU:65, one launch (start us, length us, event | category | flops | bytes accessed | tf_op | source)
XLA Modules:
  0.0 457.2 jit_solution(10752953261166834178)
XLA Ops:
  7.5 17.9 %collective-permute-start.3 = (f32[8,4,2048]{2,1,0:T(4,128)S(1)}, f32[8,4,2048]{2,1,0:T(4,128)S(1)}, u32[]{:S(2)}, u32[]{:S(2)}) collective-permute-start(f32[8,4,2048]{2,1,0:T(4,128)S(1)} %get-tuple-element.306), channel_id=1, source_target_pairs={{1,0},{2,1},{3,2},{4,3},{5,4},{6,5},{7,6},{8,7},{9,8},{10,9},{11,1... | collective-permute-start | bytes 786440 | tf_op jit(solution)/shard_map/ppermute | solution.py:29
  25.5 4.0 collective-permute-done.2
  32.5 160.5 %while.15 = (s32[]{:T(128)}, f32[5,8,2048]{2,1,0:T(8,128)}, f32[3,8,2048]{2,1,0:T(8,128)S(1)}, pred[]{:T(512)}, f32[2,16,2048]{2,1,0:T(8,128)S(1)}, /*index=5*/f...) while((s32[]{:T(128)}, f32[5,8,2048]{2,1,0:T(8,128)}, ...), condition=%wide.region_3.4_spmd.clone.clone.clone, body=%wide.region_0.3_spmd.sunk.clone.clone.clone.sunk | while | flops 4530180 | bytes 15696172 | solution.py:191
  33.7 9.5 %collective-permute-start = (f32[5,4,2048]{2,1,0:T(4,128)S(1)}, f32[5,4,2048]{2,1,0:T(4,128)S(1)}, u32[]{:S(2)}, u32[]{:S(2)}) collective-permute-start(f32[5,4,2048]{2,1,0:T(4,128)S(1)} %get-tuple-element.374), channel_id=1, source_target_pairs={{1,0},{2,1},{3,2},{4,3},{5,4},{6,5},{7,6},{8,7},{9,8},{10,9},{11,1... | collective-permute-start | bytes 491528 | tf_op jit(solution)/shard_map/while/body/eval_jaxpr/ppermute | solution.py:29
  45.5 9.3 %collective-permute-done.1 = f32[5,4,2048]{2,1,0:T(4,128)S(1)} collective-permute-done((f32[5,4,2048]{2,1,0:T(4,128)S(1)}, f32[5,4,2048]{2,1,0:T(4,128)S(1)}, u32[]{:S(2)}, u32[]{:S(2)}) %collective-permute-start.1) | collective-permute-done | bytes 163872 | tf_op jit(solution)/shard_map/while/body/eval_jaxpr/ppermute | solution.py:26
  55.8 3.1 conditional.10
  62.1 3.4 collective-permute-start.1
  66.3 7.4 %collective-permute-done.1 = f32[5,4,2048]{2,1,0:T(4,128)S(1)} collective-permute-done((f32[5,4,2048]{2,1,0:T(4,128)S(1)}, f32[5,4,2048]{2,1,0:T(4,128)S(1)}, u32[]{:S(2)}, u32[]{:S(2)}) %collective-permute-start.1) | collective-permute-done | bytes 163872 | tf_op jit(solution)/shard_map/while/body/eval_jaxpr/ppermute | solution.py:26
  74.7 3.1 conditional.10
  81.0 3.4 collective-permute-start.1
  85.2 7.4 %collective-permute-done.1 = f32[5,4,2048]{2,1,0:T(4,128)S(1)} collective-permute-done((f32[5,4,2048]{2,1,0:T(4,128)S(1)}, f32[5,4,2048]{2,1,0:T(4,128)S(1)}, u32[]{:S(2)}, u32[]{:S(2)}) %collective-permute-start.1) | collective-permute-done | bytes 163872 | tf_op jit(solution)/shard_map/while/body/eval_jaxpr/ppermute | solution.py:26
  93.6 3.1 conditional.10
  99.9 3.4 collective-permute-start.1
  104.3 7.1 %collective-permute-done.1 = f32[5,4,2048]{2,1,0:T(4,128)S(1)} collective-permute-done((f32[5,4,2048]{2,1,0:T(4,128)S(1)}, f32[5,4,2048]{2,1,0:T(4,128)S(1)}, u32[]{:S(2)}, u32[]{:S(2)}) %collective-permute-start.1) | collective-permute-done | bytes 163872 | tf_op jit(solution)/shard_map/while/body/eval_jaxpr/ppermute | solution.py:26
  112.5 3.1 conditional.10
  118.8 3.4 collective-permute-start.1
  124.7 7.4 %collective-permute-done.1 = f32[5,4,2048]{2,1,0:T(4,128)S(1)} collective-permute-done((f32[5,4,2048]{2,1,0:T(4,128)S(1)}, f32[5,4,2048]{2,1,0:T(4,128)S(1)}, u32[]{:S(2)}, u32[]{:S(2)}) %collective-permute-start.1) | collective-permute-done | bytes 163872 | tf_op jit(solution)/shard_map/while/body/eval_jaxpr/ppermute | solution.py:26
  133.2 3.1 conditional.10
  139.5 3.4 collective-permute-start.1
  143.6 7.4 %collective-permute-done.1 = f32[5,4,2048]{2,1,0:T(4,128)S(1)} collective-permute-done((f32[5,4,2048]{2,1,0:T(4,128)S(1)}, f32[5,4,2048]{2,1,0:T(4,128)S(1)}, u32[]{:S(2)}, u32[]{:S(2)}) %collective-permute-start.1) | collective-permute-done | bytes 163872 | tf_op jit(solution)/shard_map/while/body/eval_jaxpr/ppermute | solution.py:26
  152.1 3.1 conditional.10
  158.3 3.4 collective-permute-start.1
  162.5 7.4 %collective-permute-done.1 = f32[5,4,2048]{2,1,0:T(4,128)S(1)} collective-permute-done((f32[5,4,2048]{2,1,0:T(4,128)S(1)}, f32[5,4,2048]{2,1,0:T(4,128)S(1)}, u32[]{:S(2)}, u32[]{:S(2)}) %collective-permute-start.1) | collective-permute-done | bytes 163872 | tf_op jit(solution)/shard_map/while/body/eval_jaxpr/ppermute | solution.py:26
  170.9 3.1 conditional.10
  177.2 3.4 collective-permute-start.1
  181.4 7.4 %collective-permute-done.1 = f32[5,4,2048]{2,1,0:T(4,128)S(1)} collective-permute-done((f32[5,4,2048]{2,1,0:T(4,128)S(1)}, f32[5,4,2048]{2,1,0:T(4,128)S(1)}, u32[]{:S(2)}, u32[]{:S(2)}) %collective-permute-start.1) | collective-permute-done | bytes 163872 | tf_op jit(solution)/shard_map/while/body/eval_jaxpr/ppermute | solution.py:26
  193.7 6.0 %conditional.3 = (f32[3,32768]{0,1:T(8,128)}) conditional(s32[]{:T(128)} %convert_element_type.31, () %tuple.38, (s32[2,8,2048]{2,1,0:T(8,128)S(1)}, f32[3,8,2048]{2,1,0:T(8,128)}, s32[2,8,2048]{2,1,0:T(8,128)S(1)}) %tuple.122), branch_computations={%region_4.5_spmd, %region_5.7_spmd} | conditional | flops 262144 | bytes 2686988 | solution.py:201
  193.7 6.0 %broadcast.141 = f32[3,32768]{0,1:T(8,128)} broadcast(f32[]{:T(128)} %constant.39.clone), dimensions={} | broadcast | bytes 393220 | tf_op jit(solution)/shard_map/broadcast.49
  199.7 9.5 %copy.17 = f32[3,32768]{1,0:T(4,128)S(1)} copy(f32[3,32768]{0,1:T(8,128)} %get-tuple-element.427) | data formatting | bytes 786432 | tf_op jit(solution)/shard_map/cond | solution.py:201
  210.5 228.0 %collective-permute-done.4 = f32[3,32768]{1,0:T(4,128)S(1)} collective-permute-done((f32[3,32768]{1,0:T(4,128)S(1)}, f32[3,32768]{1,0:T(4,128)S(1)}, u32[]{:S(2)}, u32[]{:S(2)}) %collective-permute-start.4) | collective-permute-done | bytes 393248 | tf_op jit(solution)/shard_map/ppermute | solution.py:37
  440.4 13.1 %collective-permute-done.5 = f32[3,16384]{1,0:T(4,128)S(1)} collective-permute-done((f32[3,16384]{1,0:T(4,128)S(1)}, f32[3,16384]{1,0:T(4,128)S(1)}, u32[]{:S(2)}, u32[]{:S(2)}) %collective-permute-start.5) | collective-permute-done | bytes 196640 | tf_op jit(solution)/shard_map/ppermute | solution.py:43
  453.6 3.7 conditional.4
  (122 shorter events, 86.6 us)
Async XLA Ops:
  4.4 25.1 %collective-permute-start.2 = (f32[8,4,2048]{2,1,0:T(4,128)S(1)}, f32[8,4,2048]{2,1,0:T(4,128)S(1)}, u32[]{:S(2)}, u32[]{:S(2)}) collective-permute-start(f32[8,4,2048]{2,1,0:T(4,128)S(1)} %get-tuple-element.305), channel_id=1, source_target_pairs={{0,1},{1,2},{2,3},{3,4},{4,5},{5,6},{6,7},{7,8},{8,9},{9,10},{10,1... | collective-permute-start | bytes 786440 | tf_op jit(solution)/shard_map/ppermute | solution.py:26
  7.5 22.9 %collective-permute-start.3 = (f32[8,4,2048]{2,1,0:T(4,128)S(1)}, f32[8,4,2048]{2,1,0:T(4,128)S(1)}, u32[]{:S(2)}, u32[]{:S(2)}) collective-permute-start(f32[8,4,2048]{2,1,0:T(4,128)S(1)} %get-tuple-element.306), channel_id=1, source_target_pairs={{1,0},{2,1},{3,2},{4,3},{5,4},{6,5},{7,6},{8,7},{9,8},{10,9},{11,1... | collective-permute-start | bytes 786440 | tf_op jit(solution)/shard_map/ppermute | solution.py:29
  32.5 161.2 %copy-start = (s32[2,8,2048]{2,1,0:T(8,128)S(1)}, s32[2,8,2048]{2,1,0:T(8,128)}, u32[]{:S(2)}) copy-start(s32[2,8,2048]{2,1,0:T(8,128)} %param.20) | copy-start | bytes 393220
  32.5 161.2 %copy-start.1 = (s32[2,8,2048]{2,1,0:T(8,128)S(1)}, s32[2,8,2048]{2,1,0:T(8,128)}, u32[]{:S(2)}) copy-start(s32[2,8,2048]{2,1,0:T(8,128)} %param.21) | copy-start | bytes 393220
  33.7 11.8 %collective-permute-start = (f32[5,4,2048]{2,1,0:T(4,128)S(1)}, f32[5,4,2048]{2,1,0:T(4,128)S(1)}, u32[]{:S(2)}, u32[]{:S(2)}) collective-permute-start(f32[5,4,2048]{2,1,0:T(4,128)S(1)} %get-tuple-element.374), channel_id=1, source_target_pairs={{1,0},{2,1},{3,2},{4,3},{5,4},{6,5},{7,6},{8,7},{9,8},{10,9},{11,1... | collective-permute-start | bytes 491528 | tf_op jit(solution)/shard_map/while/body/eval_jaxpr/ppermute | solution.py:29
  43.3 11.5 %collective-permute-start.1 = (f32[5,4,2048]{2,1,0:T(4,128)S(1)}, f32[5,4,2048]{2,1,0:T(4,128)S(1)}, u32[]{:S(2)}, u32[]{:S(2)}) collective-permute-start(f32[5,4,2048]{2,1,0:T(4,128)S(1)} %get-tuple-element.375), channel_id=1, source_target_pairs={{0,1},{1,2},{2,3},{3,4},{4,5},{5,6},{6,7},{7,8},{8,9},{9,10},{10,1... | collective-permute-start | bytes 491528 | tf_op jit(solution)/shard_map/while/body/eval_jaxpr/ppermute | solution.py:26
  60.2 6.1 %collective-permute-start = (f32[5,4,2048]{2,1,0:T(4,128)S(1)}, f32[5,4,2048]{2,1,0:T(4,128)S(1)}, u32[]{:S(2)}, u32[]{:S(2)}) collective-permute-start(f32[5,4,2048]{2,1,0:T(4,128)S(1)} %get-tuple-element.374), channel_id=1, source_target_pairs={{1,0},{2,1},{3,2},{4,3},{5,4},{6,5},{7,6},{8,7},{9,8},{10,9},{11,1... | collective-permute-start | bytes 491528 | tf_op jit(solution)/shard_map/while/body/eval_jaxpr/ppermute | solution.py:29
  62.1 11.5 %collective-permute-start.1 = (f32[5,4,2048]{2,1,0:T(4,128)S(1)}, f32[5,4,2048]{2,1,0:T(4,128)S(1)}, u32[]{:S(2)}, u32[]{:S(2)}) collective-permute-start(f32[5,4,2048]{2,1,0:T(4,128)S(1)} %get-tuple-element.375), channel_id=1, source_target_pairs={{0,1},{1,2},{2,3},{3,4},{4,5},{5,6},{6,7},{7,8},{8,9},{9,10},{10,1... | collective-permute-start | bytes 491528 | tf_op jit(solution)/shard_map/while/body/eval_jaxpr/ppermute | solution.py:26
  79.1 6.1 %collective-permute-start = (f32[5,4,2048]{2,1,0:T(4,128)S(1)}, f32[5,4,2048]{2,1,0:T(4,128)S(1)}, u32[]{:S(2)}, u32[]{:S(2)}) collective-permute-start(f32[5,4,2048]{2,1,0:T(4,128)S(1)} %get-tuple-element.374), channel_id=1, source_target_pairs={{1,0},{2,1},{3,2},{4,3},{5,4},{6,5},{7,6},{8,7},{9,8},{10,9},{11,1... | collective-permute-start | bytes 491528 | tf_op jit(solution)/shard_map/while/body/eval_jaxpr/ppermute | solution.py:29
  81.0 11.5 %collective-permute-start.1 = (f32[5,4,2048]{2,1,0:T(4,128)S(1)}, f32[5,4,2048]{2,1,0:T(4,128)S(1)}, u32[]{:S(2)}, u32[]{:S(2)}) collective-permute-start(f32[5,4,2048]{2,1,0:T(4,128)S(1)} %get-tuple-element.375), channel_id=1, source_target_pairs={{0,1},{1,2},{2,3},{3,4},{4,5},{5,6},{6,7},{7,8},{8,9},{9,10},{10,1... | collective-permute-start | bytes 491528 | tf_op jit(solution)/shard_map/while/body/eval_jaxpr/ppermute | solution.py:26
  98.0 6.4 %collective-permute-start = (f32[5,4,2048]{2,1,0:T(4,128)S(1)}, f32[5,4,2048]{2,1,0:T(4,128)S(1)}, u32[]{:S(2)}, u32[]{:S(2)}) collective-permute-start(f32[5,4,2048]{2,1,0:T(4,128)S(1)} %get-tuple-element.374), channel_id=1, source_target_pairs={{1,0},{2,1},{3,2},{4,3},{5,4},{6,5},{7,6},{8,7},{9,8},{10,9},{11,1... | collective-permute-start | bytes 491528 | tf_op jit(solution)/shard_map/while/body/eval_jaxpr/ppermute | solution.py:29
  99.9 11.5 %collective-permute-start.1 = (f32[5,4,2048]{2,1,0:T(4,128)S(1)}, f32[5,4,2048]{2,1,0:T(4,128)S(1)}, u32[]{:S(2)}, u32[]{:S(2)}) collective-permute-start(f32[5,4,2048]{2,1,0:T(4,128)S(1)} %get-tuple-element.375), channel_id=1, source_target_pairs={{0,1},{1,2},{2,3},{3,4},{4,5},{5,6},{6,7},{7,8},{8,9},{9,10},{10,1... | collective-permute-start | bytes 491528 | tf_op jit(solution)/shard_map/while/body/eval_jaxpr/ppermute | solution.py:26
  116.8 7.9 %collective-permute-start = (f32[5,4,2048]{2,1,0:T(4,128)S(1)}, f32[5,4,2048]{2,1,0:T(4,128)S(1)}, u32[]{:S(2)}, u32[]{:S(2)}) collective-permute-start(f32[5,4,2048]{2,1,0:T(4,128)S(1)} %get-tuple-element.374), channel_id=1, source_target_pairs={{1,0},{2,1},{3,2},{4,3},{5,4},{6,5},{7,6},{8,7},{9,8},{10,9},{11,1... | collective-permute-start | bytes 491528 | tf_op jit(solution)/shard_map/while/body/eval_jaxpr/ppermute | solution.py:29
  118.8 13.3 %collective-permute-start.1 = (f32[5,4,2048]{2,1,0:T(4,128)S(1)}, f32[5,4,2048]{2,1,0:T(4,128)S(1)}, u32[]{:S(2)}, u32[]{:S(2)}) collective-permute-start(f32[5,4,2048]{2,1,0:T(4,128)S(1)} %get-tuple-element.375), channel_id=1, source_target_pairs={{0,1},{1,2},{2,3},{3,4},{4,5},{5,6},{6,7},{7,8},{8,9},{9,10},{10,1... | collective-permute-start | bytes 491528 | tf_op jit(solution)/shard_map/while/body/eval_jaxpr/ppermute | solution.py:26
  137.5 6.1 %collective-permute-start = (f32[5,4,2048]{2,1,0:T(4,128)S(1)}, f32[5,4,2048]{2,1,0:T(4,128)S(1)}, u32[]{:S(2)}, u32[]{:S(2)}) collective-permute-start(f32[5,4,2048]{2,1,0:T(4,128)S(1)} %get-tuple-element.374), channel_id=1, source_target_pairs={{1,0},{2,1},{3,2},{4,3},{5,4},{6,5},{7,6},{8,7},{9,8},{10,9},{11,1... | collective-permute-start | bytes 491528 | tf_op jit(solution)/shard_map/while/body/eval_jaxpr/ppermute | solution.py:29
  139.5 11.5 %collective-permute-start.1 = (f32[5,4,2048]{2,1,0:T(4,128)S(1)}, f32[5,4,2048]{2,1,0:T(4,128)S(1)}, u32[]{:S(2)}, u32[]{:S(2)}) collective-permute-start(f32[5,4,2048]{2,1,0:T(4,128)S(1)} %get-tuple-element.375), channel_id=1, source_target_pairs={{0,1},{1,2},{2,3},{3,4},{4,5},{5,6},{6,7},{7,8},{8,9},{9,10},{10,1... | collective-permute-start | bytes 491528 | tf_op jit(solution)/shard_map/while/body/eval_jaxpr/ppermute | solution.py:26
  156.4 6.1 %collective-permute-start = (f32[5,4,2048]{2,1,0:T(4,128)S(1)}, f32[5,4,2048]{2,1,0:T(4,128)S(1)}, u32[]{:S(2)}, u32[]{:S(2)}) collective-permute-start(f32[5,4,2048]{2,1,0:T(4,128)S(1)} %get-tuple-element.374), channel_id=1, source_target_pairs={{1,0},{2,1},{3,2},{4,3},{5,4},{6,5},{7,6},{8,7},{9,8},{10,9},{11,1... | collective-permute-start | bytes 491528 | tf_op jit(solution)/shard_map/while/body/eval_jaxpr/ppermute | solution.py:29
  158.3 11.5 %collective-permute-start.1 = (f32[5,4,2048]{2,1,0:T(4,128)S(1)}, f32[5,4,2048]{2,1,0:T(4,128)S(1)}, u32[]{:S(2)}, u32[]{:S(2)}) collective-permute-start(f32[5,4,2048]{2,1,0:T(4,128)S(1)} %get-tuple-element.375), channel_id=1, source_target_pairs={{0,1},{1,2},{2,3},{3,4},{4,5},{5,6},{6,7},{7,8},{8,9},{9,10},{10,1... | collective-permute-start | bytes 491528 | tf_op jit(solution)/shard_map/while/body/eval_jaxpr/ppermute | solution.py:26
  175.3 6.1 %collective-permute-start = (f32[5,4,2048]{2,1,0:T(4,128)S(1)}, f32[5,4,2048]{2,1,0:T(4,128)S(1)}, u32[]{:S(2)}, u32[]{:S(2)}) collective-permute-start(f32[5,4,2048]{2,1,0:T(4,128)S(1)} %get-tuple-element.374), channel_id=1, source_target_pairs={{1,0},{2,1},{3,2},{4,3},{5,4},{6,5},{7,6},{8,7},{9,8},{10,9},{11,1... | collective-permute-start | bytes 491528 | tf_op jit(solution)/shard_map/while/body/eval_jaxpr/ppermute | solution.py:29
  177.2 11.5 %collective-permute-start.1 = (f32[5,4,2048]{2,1,0:T(4,128)S(1)}, f32[5,4,2048]{2,1,0:T(4,128)S(1)}, u32[]{:S(2)}, u32[]{:S(2)}) collective-permute-start(f32[5,4,2048]{2,1,0:T(4,128)S(1)} %get-tuple-element.375), channel_id=1, source_target_pairs={{0,1},{1,2},{2,3},{3,4},{4,5},{5,6},{6,7},{7,8},{8,9},{9,10},{10,1... | collective-permute-start | bytes 491528 | tf_op jit(solution)/shard_map/while/body/eval_jaxpr/ppermute | solution.py:26
  209.2 229.3 %collective-permute-start.4 = (f32[3,32768]{1,0:T(4,128)S(1)}, f32[3,32768]{1,0:T(4,128)S(1)}, u32[]{:S(2)}, u32[]{:S(2)}) collective-permute-start(f32[3,32768]{1,0:T(4,128)S(1)} %copy.17), channel_id=1, source_target_pairs={{0,512},{1,513},{2,514},{3,515},{4,516},{5,517},{6,518},{7,519},{8... | collective-permute-start | bytes 1179656 | tf_op jit(solution)/shard_map/ppermute | solution.py:37
  438.5 15.1 %collective-permute-start.5 = (f32[3,16384]{1,0:T(4,128)S(1)}, f32[3,16384]{1,0:T(4,128)S(1)}, u32[]{:S(2)}, u32[]{:S(2)}) collective-permute-start(f32[3,16384]{1,0:T(4,128)S(1)} %slice.432), channel_id=1, source_target_pairs={{0,1},{1,2},{2,3},{3,4},{4,5},{5,6},{6,7},{7,8},{8,9},{9,10},{10,1... | collective-permute-start | bytes 589832 | tf_op jit(solution)/shard_map/ppermute | solution.py:43
where the time goes:
time: 460 us; the launch traced here: 457 us
  waiting for transfers between devices  314 us (68%)
  starting transfers between devices  72.7 us (16%)
  other arithmetic  39.1 us (8%)
  local copies, waits for them, and re-layouts  29.5 us (6%)
    ppermute x1, waiting for transfers between devices, shifted(): lax.ppermute(value, axis, [(source, source + steps) for source in range(f...  228 us
    ppermute x9, waiting for transfers between devices, extended_2(): lax.ppermute(lax.slice_in_dim(block, block.shape[dim] - width, None, axis...  64.5 us
    ppermute x9, starting transfers between devices, extended_2(): lax.ppermute(lax.slice_in_dim(block, 0, width, axis=dim), axis, backward)  40.9 us
    ppermute x9, starting transfers between devices, extended_2(): lax.ppermute(lax.slice_in_dim(block, block.shape[dim] - width, None, axis...  28.6 us
    sub x16, other arithmetic, ocean_step(): return centre - courant * change  23.4 us
    ppermute x1, waiting for transfers between devices, from_behind(): return lax.ppermute(value, axis, pairs)  13.1 us
    concatenate x9, other arithmetic, extended_2(): block = jnp.concatenate([low, block, high], axis=dim)  9.76 us
    cond x1, local copies, waits for them, and re-layouts, body(): partial_sums = lax.cond(is_ice, window_sums, no_window, average)  9.46 us
  transfers between devices with their start and end apart: 20, of which 20 were waited for; matrix products, arithmetic and copies ran while one was open for 0% of the time, Pallas kernels for 0%

commit v1 on v0

v1 whole, which is shorter than its diff:
```python
import functools
import jax
import jax.numpy as jnp
from jax import lax
from jax.experimental import pallas as pl
from jax.experimental.pallas import tpu as pltpu
from jax.sharding import PartitionSpec as P

LEVELS = (1.0, 0.8, 0.6, 0.45, 0.3)
OWN = 8
RB = 32
LANE = 128
MESH = pl.DeviceIdType.MESH
UP, DOWN = 0, 1


def own(ref, *lead):
    return ref.at[lead + (slice(None),) * (len(ref.shape) - 2 - len(lead)) + (pl.ds(OWN, 8), slice(None))]


def kernel(n, nt, init, forcing, current, cover, targets, weights, state_out, coupled_out,
           S, W, T, F, CUR, COV, TG, WT, TOT, VALS, TH, TL, ACC, FLUX, RECVW, RECVA,
           load_sem, send_sem, recv_sem, st_send, st_recv, a_send, a_recv, w_send, w_recv, out_sem, gate):
    comp = lax.axis_index("comp")
    b = lax.axis_index("blk")
    is_ice = comp == 0
    has_up = b > 0
    has_down = b < n - 1
    nxt = lax.rem(b + 1, n)
    prv = lax.rem(b + n - 1, n)

    loads = [
        pltpu.make_async_copy(init, S.at[0, :, :, pl.ds(OWN, 8), :], load_sem.at[0]),
        pltpu.make_async_copy(forcing, F, load_sem.at[1]),
        pltpu.make_async_copy(current, CUR.at[:, :, pl.ds(OWN, 8), :], load_sem.at[2]),
        pltpu.make_async_copy(cover, COV, load_sem.at[3]),
        pltpu.make_async_copy(targets, TG, load_sem.at[4]),
        pltpu.make_async_copy(weights, WT, load_sem.at[5]),
    ]
    for c in loads:
        c.start()

    def zero_halo(lo):
        z5 = jnp.zeros((5, nt, 8, LANE), jnp.float32)
        for q in range(2):
            S[q, :, :, pl.ds(lo, 8), :] = z5
        T[:, :, pl.ds(lo, 8), :] = z5
        CUR[:, :, pl.ds(lo, 8), :] = jnp.zeros((2, nt, 8, LANE), jnp.float32)

    @pl.when(jnp.logical_not(has_up))
    def _():
        zero_halo(0)

    @pl.when(jnp.logical_not(has_down))
    def _():
        zero_halo(16)

    z5 = jnp.zeros((5, nt, 8, LANE), jnp.float32)
    for q in range(2):
        S[q, :, :, pl.ds(24, 8), :] = z5
    T[:, :, pl.ds(24, 8), :] = z5
    W[:, :, pl.ds(0, 8), :] = z5
    W[:, :, pl.ds(24, 8), :] = z5
    CUR[:, :, pl.ds(24, 8), :] = jnp.zeros((2, nt, 8, LANE), jnp.float32)
    TOT[...] = jnp.zeros((3, nt, 8, LANE), jnp.float32)

    barrier = pltpu.get_barrier_semaphore()

    @pl.when(has_up)
    def _():
        pl.semaphore_signal(barrier, inc=1, device_id=(comp, b - 1), device_id_type=MESH)

    @pl.when(has_down)
    def _():
        pl.semaphore_signal(barrier, inc=1, device_id=(comp, b + 1), device_id_type=MESH)

    pl.semaphore_signal(barrier, inc=1, device_id=(1 - comp, b), device_id_type=MESH)

    @pl.when(is_ice)
    def _():
        pl.semaphore_signal(barrier, inc=1, device_id=(1, nxt), device_id_type=MESH)

    @pl.when(jnp.logical_not(is_ice))
    def _():
        pl.semaphore_signal(barrier, inc=1, device_id=(0, prv), device_id_type=MESH)

    pl.semaphore_wait(barrier, 2 + has_up.astype(jnp.int32) + has_down.astype(jnp.int32))

    def remote(src, dst, ss, rs, dev):
        return pltpu.make_async_remote_copy(src_ref=src, dst_ref=dst, send_sem=ss, recv_sem=rs,
                                            device_id=dev, device_id_type=MESH)

    def state_copy(d, q, src=None):
        src = S.at[q, :, :, pl.ds(OWN, 8), :] if src is None else src
        lo, dev = (16, (comp, b - 1)) if d == UP else (0, (comp, b + 1))
        return remote(src, S.at[q, :, :, pl.ds(lo, 8), :], send_sem.at[d, q], recv_sem.at[d, q], dev)

    def ice_static_copy(d):
        lo, dev = (16, (comp, b - 1)) if d == UP else (0, (comp, b + 1))
        return remote(T.at[pl.ds(0, 4), :, pl.ds(OWN, 8), :], T.at[pl.ds(0, 4), :, pl.ds(lo, 8), :],
                      st_send.at[d], st_recv.at[d], dev)

    def ocean_static_copy(d):
        lo, dev = (16, (comp, b - 1)) if d == UP else (0, (comp, b + 1))
        return remote(current, CUR.at[:, :, pl.ds(lo, 8), :], st_send.at[d], st_recv.at[d], dev)

    def both(make, what):
        pairs = ((UP, has_up, has_down), (DOWN, has_down, has_up))
        for d, sends, receives in pairs:
            @pl.when(receives if what == "recv" else sends)
            def _():
                c = make(d)
                if what == "start":
                    c.start()
                elif what == "recv":
                    c.wait_recv()
                else:
                    c.wait_send()

    lane = lax.broadcasted_iota(jnp.int32, (nt, 8, LANE), 2)
    first = lane == 0
    last = lane == LANE - 1
    zt = jnp.zeros((1, 8, LANE), jnp.float32)

    def right_of(x):
        u = pltpu.roll(x, LANE - 1, 2)
        return jnp.where(last, jnp.concatenate([u[1:], zt], 0), u)

    def left_of(x):
        u = pltpu.roll(x, 1, 2)
        return jnp.where(first, jnp.concatenate([zt, u[:-1]], 0), u)

    def dcol(x):
        return right_of(x) - left_of(x)

    avg_copy = remote(TOT, RECVA, a_send, a_recv, (1, b))
    win_copy = remote(FLUX, RECVW, w_send, w_recv, (1, nxt))

    def scatter(avg_ref, base):
        for k in range(2):
            t = TG[k]
            row = lax.shift_right_logical(t, 11) - base
            cell = lax.bitwise_and(lax.shift_right_logical(t, 8), 7) * 8 + row
            inside = jnp.logical_and(row >= 0, row < 8)
            TH[k] = jnp.where(inside, cell, 255).astype(jnp.float32)
            TL[k] = lax.bitwise_and(t, 255).astype(jnp.float32)
            w = WT[k].astype(jnp.float32) * 0.25
            for ch in range(3):
                v = avg_ref[ch] * w
                hi = v.astype(jnp.bfloat16).astype(jnp.float32)
                VALS[k, 2 * ch] = hi
                VALS[k, 2 * ch + 1] = v - hi
        ACC[...] = jnp.zeros_like(ACC)
        iota = lax.broadcasted_iota(jnp.int32, (16, LANE), 0).astype(jnp.float32)

        def rows16(ref, k, *idx):
            return jnp.broadcast_to(ref[(k,) + idx], (16, LANE)).astype(jnp.bfloat16)

        zero = jnp.zeros((16, LANE), jnp.bfloat16)
        one = jnp.ones((16, LANE), jnp.bfloat16)
        iotas = [(iota + 16.0 * g).astype(jnp.bfloat16) for g in range(16)]

        def body(i, carry):
            k = i // 8
            r = i % 8
            total = None
            for jj in range(nt // 2):
                lhs_halves, rhs_halves = [], []
                for j in (2 * jj, 2 * jj + 1):
                    th = rows16(TH, k, j, pl.ds(r, 1), slice(None))
                    tl = rows16(TL, k, j, pl.ds(r, 1), slice(None))
                    masks = [th == iotas[g] for g in range(4)]
                    parts = []
                    for m in range(6):
                        v = rows16(VALS, k, m, j, pl.ds(r, 1), slice(None))
                        parts += [jnp.where(masks[g], v, zero) for g in range(4)]
                    lhs_halves.append(jnp.concatenate(parts, 0))
                    rhs_halves.append(jnp.concatenate([jnp.where(tl == iotas[g], one, zero) for g in range(16)], 0))
                lhs = jnp.concatenate(lhs_halves, 1)
                rhs = jnp.concatenate(rhs_halves, 1)
                part = lax.dot_general(lhs, rhs, (((1,), (1,)), ((), ())), preferred_element_type=jnp.float32)
                total = part if total is None else total + part
            ACC[...] += total
            return carry

        lax.fori_loop(0, 16, body, 0)
        for ch in range(3):
            for cb in range(nt // 2):
                for h in range(2):
                    FLUX[ch, 2 * cb + h] = (
                        ACC[pl.ds((2 * ch) * 64 + 8 * cb, 8), pl.ds(LANE * h, LANE)]
                        + ACC[pl.ds((2 * ch + 1) * 64 + 8 * cb, 8), pl.ds(LANE * h, LANE)]
                    )

    out_state = pltpu.make_async_copy(S.at[0, :, :, pl.ds(OWN, 8), :], state_out, out_sem.at[0])
    out_total = pltpu.make_async_copy(TOT, coupled_out, out_sem.at[1])
    out_flux = pltpu.make_async_copy(FLUX, coupled_out, out_sem.at[1])

    @pl.when(is_ice)
    def ice():
        both(lambda d: state_copy(d, 0, init), "start")
        loads[1].wait()
        loads[2].wait()
        loads[3].wait()
        cov = COV[...].astype(jnp.float32)
        inv = cov / (4.0 * F[0] + 1.0)
        T[0, :, pl.ds(OWN, 8), :] = F[1] * cov * (1.0 / 3.0)
        T[1, :, pl.ds(OWN, 8), :] = inv
        for x in range(2):
            T[2 + x, :, pl.ds(OWN, 8), :] = inv * (F[2 + x] + CUR[x, :, pl.ds(OWN, 8), :])
        both(ice_static_copy, "start")
        loads[0].wait()
        both(ice_static_copy, "recv")
        for lo in (0, 8, 16):
            inv = T[1, :, pl.ds(lo, 8), :]
            T[4, :, pl.ds(lo, 8), :] = jnp.where(inv > 0.0, 1.0 - inv, 0.0)

        def stress(q, s):
            vx_lo, vx_hi = S[q, 0, :, pl.ds(s - 1, 8), :], S[q, 0, :, pl.ds(s + 1, 8), :]
            vy_lo, vy_hi = S[q, 1, :, pl.ds(s - 1, 8), :], S[q, 1, :, pl.ds(s + 1, 8), :]
            a = vx_hi - vx_lo
            c = dcol(S[q, 1, :, pl.ds(s, 8), :])
            sh = dcol(S[q, 0, :, pl.ds(s, 8), :]) + (vy_hi - vy_lo)
            dd = a + c
            tt = a - c
            p = T[0, :, pl.ds(s, 8), :]
            w = p * lax.rsqrt(4.0 * (dd * dd) + (tt * tt + sh * sh) + 0.16)
            third = 2.0 / 3.0
            S[q, 2, :, pl.ds(s, 8), :] = third * S[q, 2, :, pl.ds(s, 8), :] + (2.0 * (w * dd) - p)
            S[q, 3, :, pl.ds(s, 8), :] = third * S[q, 3, :, pl.ds(s, 8), :] + 0.5 * (w * tt)
            S[q, 4, :, pl.ds(s, 8), :] = third * S[q, 4, :, pl.ds(s, 8), :] + 0.25 * (w * sh)

        def velocity(q, s, to):
            def at(f, o):
                return S[q, f, :, pl.ds(s + o, 8), :]
            fx = 0.25 * ((at(2, 1) + at(3, 1)) - (at(2, -1) + at(3, -1))) + 0.5 * dcol(at(4, 0))
            fy = 0.5 * (at(4, 1) - at(4, -1)) + 0.25 * dcol(at(2, 0) - at(3, 0))
            vx, vy = at(0, 0), at(1, 0)
            ca, cb = T[4, :, pl.ds(s, 8), :], T[1, :, pl.ds(s, 8), :]
            S[to, 0, :, pl.ds(s, 8), :] = ca * (vx + 0.1 * vy) + cb * fx + T[2, :, pl.ds(s, 8), :]
            S[to, 1, :, pl.ds(s, 8), :] = ca * (vy - 0.1 * vx) + cb * fy + T[3, :, pl.ds(s, 8), :]

        def add_total(q):
            vx, vy = S[q, 0, :, pl.ds(OWN, 8), :], S[q, 1, :, pl.ds(OWN, 8), :]
            TOT[0] += vx
            TOT[1] += vy
            TOT[2] += jnp.sqrt(1.0 + vx * vx + vy * vy)

        def phase(p, carry):
            q = lax.rem(p, 2)
            o = 1 - q
            both(lambda d: state_copy(d, q), "recv")
            both(lambda d: state_copy(d, q), "sent")

            @pl.when(p < 2)
            def _():
                pl.semaphore_signal(gate, inc=1, device_id=(1, b), device_id_type=MESH)

            for t, (ss, vs) in enumerate((((1, 9, 17), (2, 10, 18)), ((3, 11, 19), (4, 12)),
                                          ((5, 13), (6, 14)), ((7, 15), (8,)))):
                for s in ss:
                    stress(q, s)
                for s in vs:
                    velocity(q, s, o if t == 3 else q)
                if t == 3:
                    for f in (2, 3, 4):
                        S[o, f, :, pl.ds(OWN, 8), :] = S[q, f, :, pl.ds(OWN, 8), :]
                    @pl.when(p < 3)
                    def _():
                        both(lambda d: state_copy(d, o), "start")
                add_total(o if t == 3 else q)
            return carry

        lax.fori_loop(0, 4, phase, 0)
        both(ice_static_copy, "sent")
        out_state.start()
        cov = COV[...].astype(jnp.float32)
        for x in range(2):
            TOT[x] = TOT[x] * (1.0 / 16.0) - cov * CUR[x, :, pl.ds(OWN, 8), :]
        TOT[2] = TOT[2] * (cov * F[4] * (1.0 / 16.0))
        avg_copy.start()
        out_total.start()
        loads[4].wait()
        loads[5].wait()
        scatter(TOT, 8)
        win_copy.start()
        avg_copy.wait_send()
        out_state.wait()
        out_total.wait()
        win_copy.wait_send()

    @pl.when(jnp.logical_not(is_ice))
    def ocean():
        loads[2].wait()
        pl.semaphore_wait(gate, 1)
        both(lambda d: state_copy(d, 0, init), "start")
        both(ocean_static_copy, "start")
        loads[0].wait()
        loads[1].wait()
        loads[3].wait()
        both(ocean_static_copy, "recv")

        def level(src, dst, l, s, flow):
            px, nx, py, ny = flow
            q = src[l, :, pl.ds(s, 8), :]
            lft, rgt = left_of(q), right_of(q)
            ch = (px * (q - src[l, :, pl.ds(s - 1, 8), :]) + nx * (src[l, :, pl.ds(s + 1, 8), :] - q)
                  + py * (q - lft) + ny * (rgt - q))
            dst[l, :, pl.ds(s, 8), :] = q - (0.2 * LEVELS[l]) * ch

        def step(src, dst, starts):
            for s in starts:
                cx, cy = CUR[0, :, pl.ds(s, 8), :], CUR[1, :, pl.ds(s, 8), :]
                flow = (jnp.maximum(cx, 0.0), jnp.minimum(cx, 0.0), jnp.maximum(cy, 0.0), jnp.minimum(cy, 0.0))
                for l in range(5):
                    level(src, dst, l, s, flow)

        def phase(p, carry):
            q = lax.rem(p, 2)
            o = 1 - q

            both(lambda d: state_copy(d, q), "recv")
            both(lambda d: state_copy(d, q), "sent")
            bufs = (S.at[q], W)
            for t in range(8):
                count = 22 - 2 * t
                starts = [1 + t + 8 * g for g in range(-(-count // 8))]
                step(bufs[t % 2], S.at[o] if t == 7 else bufs[(t + 1) % 2], starts)

            @pl.when(p < 1)
            def _():
                pl.semaphore_wait(gate, 1)
                both(lambda d: state_copy(d, o), "start")

            return carry

        lax.fori_loop(0, 2, phase, 0)
        both(ocean_static_copy, "sent")
        loads[4].wait()
        loads[5].wait()
        avg_copy.wait_recv()
        scatter(RECVA, 0)
        win_copy.wait_recv()
        for ch in range(3):
            FLUX[ch] = FLUX[ch] + RECVW[ch]
        S[0, 0, :, pl.ds(OWN, 8), :] = S[0, 0, :, pl.ds(OWN, 8), :] - 0.5 * FLUX[2]
        out_state.start()
        out_flux.start()
        out_state.wait()
        out_flux.wait()


def to_tiles(x):
    lead, cols = x.shape[:-2], x.shape[-1]
    y = x.reshape(lead + (8, cols // LANE, LANE))
    return jnp.swapaxes(y, -3, -2)


def from_tiles(y):
    x = jnp.swapaxes(y, -3, -2)
    return x.reshape(x.shape[:-2] + (x.shape[-2] * LANE,))


def body(n, initial, ice_forcing, ocean_current, ice_cover, targets, weights):
    cols = initial.shape[-1]
    nt = cols // LANE
    f32 = jnp.float32
    own_t = (nt, 8, LANE)
    ext_t = (nt, RB, LANE)
    args = [to_tiles(x) for x in (initial[0], ice_forcing, ocean_current, ice_cover, targets, weights)]
    dma = pltpu.SemaphoreType.DMA
    state, coupled = pl.pallas_call(
        functools.partial(kernel, n, nt),
        out_shape=(jax.ShapeDtypeStruct((5,) + own_t, f32), jax.ShapeDtypeStruct((3,) + own_t, f32)),
        in_specs=[pl.BlockSpec(memory_space=pl.ANY)] * 6,
        out_specs=(pl.BlockSpec(memory_space=pl.ANY),) * 2,
        scratch_shapes=[
            pltpu.VMEM((2, 5) + ext_t, f32),
            pltpu.VMEM((5,) + ext_t, f32),
            pltpu.VMEM((5,) + ext_t, f32),
            pltpu.VMEM((5,) + own_t, f32),
            pltpu.VMEM((2,) + ext_t, f32),
            pltpu.VMEM(own_t, jnp.int32),
            pltpu.VMEM((2,) + own_t, jnp.int32),
            pltpu.VMEM((2,) + own_t, jnp.int32),
            pltpu.VMEM((3,) + own_t, f32),
            pltpu.VMEM((2, 6) + own_t, f32),
            pltpu.VMEM((2,) + own_t, f32),
            pltpu.VMEM((2,) + own_t, f32),
            pltpu.VMEM((384, 256), f32),
            pltpu.VMEM((3,) + own_t, f32),
            pltpu.VMEM((3,) + own_t, f32),
            pltpu.VMEM((3,) + own_t, f32),
            dma((6,)), dma((2, 2)), dma((2, 2)), dma((2,)), dma((2,)),
            dma, dma, dma, dma, dma((2,)), pltpu.SemaphoreType.REGULAR,
        ],
        compiler_params=pltpu.CompilerParams(collective_id=0, has_side_effects=True),
    )(*args)
    return from_tiles(state)[None], from_tiles(coupled)[None]


def solution(mesh):
    placed = (
        P("comp", None, "blk", None),
        P(None, "blk", None),
        P(None, "blk", None),
        P("blk", None),
        P(None, "blk", None),
        P(None, "blk", None),
    )
    return jax.shard_map(
        functools.partial(body, mesh.shape["blk"]),
        mesh=mesh,
        in_specs=placed,
        out_specs=(P("comp", None, "blk", None), P("comp", None, "blk", None)),
        check_vma=False,
    )
```

time: 460 us -> 90.5 us (0.20)
  waiting for transfers between devices: 314 us -> 0 us
  Pallas kernels: 0 us -> 87.3 us
  starting transfers between devices: 72.7 us -> 0 us
  other arithmetic: 39.1 us -> 0 us
  local copies, waits for them, and re-layouts: 29.5 us -> 2.44 us
    ppermute x20 -> x0, waiting for transfers between devices: 314 us -> none  [the longest x1 228 us: shifted(): lax.ppermute(value, axis, [(source, source + steps) for source in range(f...]
    pallas_call x0 -> x1, Pallas kernels: none -> 87.3 us  [body(): pl.pallas_call(functools.partial(kernel, n, nt), out_shape=(jax.ShapeDtyp...]
    ppermute x20 -> x0, starting transfers between devices: 72.7 us -> none  [the longest x9 40.9 us: extended_2(): lax.ppermute(lax.slice_in_dim(block, 0, width, axis=dim), axis, backward)]
    sub x17 -> x0, other arithmetic: 24.2 us -> none  [the longest x16 23.4 us: ocean_step(): return centre - courant * change]
    slice x27 -> x0, local copies, waits for them, and re-layouts: 11.1 us -> none  [the longest x9 9.28 us: extended_2(): lax.slice_in_dim(block, block.shape[dim] - width, None, axis=dim)]
    concatenate x10 -> x0, other arithmetic: 10.8 us -> none  [the longest x9 9.76 us: extended_2(): block = jnp.concatenate([low, block, high], axis=dim)]
    cond x2 -> x0, local copies, waits for them, and re-layouts: 10.3 us -> none  [the longest x1 9.46 us: body(): partial_sums = lax.cond(is_ice, window_sums, no_window, average)]
    another operation x1 -> x0, local copies, waits for them, and re-layouts: 6.01 us -> none
  transfers between devices with their start and end apart: 20 -> 0, of which waited for: 20 -> 0; matrix products, arithmetic and copies ran while one was open for 0% -> 0% of each run, Pallas kernels for 0% -> 0%
where the time goes in v1:
time: 90.5 us; the launch traced here: 90.4 us
  Pallas kernels  87.3 us (96%)
  local copies, waits for them, and re-layouts  2.44 us (3%)
    pallas_call x1, Pallas kernels, body(): pl.pallas_call(functools.partial(kernel, n, nt), out_shape=(jax.ShapeDtyp...  87.3 us
    unnamed x4, local copies, waits for them, and re-layouts  2.44 us

profile of v1, /device:TPU:65, one launch (start us, length us, event | category | flops | bytes accessed | tf_op | source)
XLA Modules:
  0.0 90.4 jit_solution(8601104730733322429)
XLA Ops:
  0.6 87.3 %shard_map.77 = (f32[5,16,8,128]{3,2,1,0:T(8,128)}, f32[3,16,8,128]{3,2,1,0:T(8,128)}) custom-call(f32[5,16,8,128]{3,2,1,0:T(8,128)} %bitcast.25, f32[5,16,8,128]{3,2,1,0:T(8,128)} %bitcast.26, f32[2,16,8,128]{3,2,1,0:T(8,128)} %bitcast.28, s32[16,8,128]{2,1,0:T(8,128)} %bitcast.31, s32[2,16,8,128]{3,2,1,0:T(8,128)} %bitcast.29, s32[2,16,8,128]{3,2,1,0:T(8,128)} %bitcast.30), custom_call_target="tpu_custom_call" | custom-call | tf_op jit(solution)/shard_map/pallas_call | solution.py:372
  87.9 0.0 copy-start
  87.9 1.8 %copy.10 = f32[1,5,8,2048]{3,2,1,0:T(8,128)} copy(f32[1,5,8,2048]{3,2,1,0:T(8,128)} %bitcast.24) | data formatting | bytes 655360
  89.7 0.0 copy-done
  89.7 0.7 copy.11
Async XLA Ops:
  87.9 1.8 %copy-start = (f32[3,16,8,128]{3,2,1,0:T(8,128)S(1)}, f32[3,16,8,128]{3,2,1,0:T(8,128)}, u32[]{:S(2)}) copy-start(f32[3,16,8,128]{3,2,1,0:T(8,128)} %get-tuple-element.5) | copy-start | bytes 589828

commit v2 on v1

v2 whole, which is shorter than its diff:
```python
import functools
import jax
import jax.numpy as jnp
from jax import lax
from jax.experimental import pallas as pl
from jax.experimental.pallas import tpu as pltpu
from jax.sharding import PartitionSpec as P

LEVELS = (1.0, 0.8, 0.6, 0.45, 0.3)
OWN = 8
RB = 32
LANE = 128
CHAINS = 3
MESH = pl.DeviceIdType.MESH
UP, DOWN = 0, 1


def kernel(n, nt, init, forcing, current, cover, targets, weights, state_out, coupled_out,
           S, Q, W, T, F, CUR, COV, TG, WT, TC, TOT, VALS, TH, TL, RHS, ACC, FLUX, RECVW, RECVA,
           load_sem, ice_send, ice_recv, q_send, q_recv, st_send, st_recv, a_send, a_recv, w_send, w_recv,
           out_sem, gate):
    comp = lax.axis_index("comp")
    b = lax.axis_index("blk")
    is_ice = comp == 0
    has_up = b > 0
    has_down = b < n - 1
    nxt = lax.rem(b + 1, n)
    prv = lax.rem(b + n - 1, n)
    step_t = (nt - 1) // CHAINS
    ct = step_t + 1

    barrier = pltpu.get_barrier_semaphore()

    @pl.when(has_up)
    def _():
        pl.semaphore_signal(barrier, inc=1, device_id=(comp, b - 1), device_id_type=MESH)

    @pl.when(has_down)
    def _():
        pl.semaphore_signal(barrier, inc=1, device_id=(comp, b + 1), device_id_type=MESH)

    pl.semaphore_signal(barrier, inc=1, device_id=(1 - comp, b), device_id_type=MESH)

    @pl.when(is_ice)
    def _():
        pl.semaphore_signal(barrier, inc=1, device_id=(1, nxt), device_id_type=MESH)

    @pl.when(jnp.logical_not(is_ice))
    def _():
        pl.semaphore_signal(barrier, inc=1, device_id=(0, prv), device_id_type=MESH)

    loads = [
        pltpu.make_async_copy(forcing, F, load_sem.at[0]),
        pltpu.make_async_copy(current, CUR.at[:, :, pl.ds(OWN, 8), :], load_sem.at[1]),
        pltpu.make_async_copy(cover, COV, load_sem.at[2]),
        pltpu.make_async_copy(targets, TG, load_sem.at[3]),
        pltpu.make_async_copy(weights, WT, load_sem.at[4]),
    ]
    ice_loads = [
        pltpu.make_async_copy(init.at[:, pl.ds(step_t * c, ct)], S.at[c, 0, :, :, pl.ds(OWN, 8), :], load_sem.at[5 + c])
        for c in range(CHAINS)
    ]
    ocean_load = pltpu.make_async_copy(init, Q.at[0, :, :, pl.ds(OWN, 8), :], load_sem.at[5])
    for c in loads:
        c.start()

    def zeros(*shape):
        return jnp.zeros(shape + (8, LANE), jnp.float32)

    def zero_rows(lo):
        @pl.when(is_ice)
        def _():
            for c in range(CHAINS):
                for q in range(2):
                    S[c, q, :, :, pl.ds(lo, 8), :] = zeros(5, ct)
            T[:, :, pl.ds(lo, 8), :] = zeros(5, nt)

        @pl.when(jnp.logical_not(is_ice))
        def _():
            for q in range(2):
                Q[q, :, :, pl.ds(lo, 8), :] = zeros(5, nt)
            CUR[:, :, pl.ds(lo, 8), :] = zeros(2, nt)

    @pl.when(jnp.logical_not(has_up))
    def _():
        zero_rows(0)

    @pl.when(jnp.logical_not(has_down))
    def _():
        zero_rows(16)

    zero_rows(24)

    def remote(src, dst, ss, rs, dev):
        return pltpu.make_async_remote_copy(src_ref=src, dst_ref=dst, send_sem=ss, recv_sem=rs,
                                            device_id=dev, device_id_type=MESH)

    def beside(d):
        return (16, (comp, b - 1)) if d == UP else (0, (comp, b + 1))

    def ice_copy(d, c, q, src=None):
        lo, dev = beside(d)
        src = S.at[c, q, :, :, pl.ds(OWN, 8), :] if src is None else src
        return remote(src, S.at[c, q, :, :, pl.ds(lo, 8), :], ice_send.at[d, c, q], ice_recv.at[d, c, q], dev)

    def ice_first(d, c):
        return ice_copy(d, c, 0, init.at[:, pl.ds(step_t * c, ct)])

    def ice_static_copy(d, c):
        lo, dev = beside(d)
        t0 = 0 if c == 0 else step_t * c + 1
        tiles = pl.ds(t0, step_t * c + ct - t0)
        return remote(T.at[pl.ds(0, 4), tiles, pl.ds(OWN, 8), :], T.at[pl.ds(0, 4), tiles, pl.ds(lo, 8), :],
                      st_send.at[d, c], st_recv.at[d, c], dev)

    def ocean_copy(d, q, src=None):
        lo, dev = beside(d)
        src = Q.at[q, :, :, pl.ds(OWN, 8), :] if src is None else src
        return remote(src, Q.at[q, :, :, pl.ds(lo, 8), :], q_send.at[d, q], q_recv.at[d, q], dev)

    def ocean_static_copy(d):
        lo, dev = beside(d)
        return remote(current, CUR.at[:, :, pl.ds(lo, 8), :], st_send.at[d, 0], st_recv.at[d, 0], dev)

    def both(make, what):
        pairs = ((UP, has_up, has_down), (DOWN, has_down, has_up))
        for d, sends, receives in pairs:
            @pl.when(receives if what == "recv" else sends)
            def _():
                c = make(d)
                if what == "start":
                    c.start()
                elif what == "recv":
                    c.wait_recv()
                else:
                    c.wait_send()

    zt = zeros(1)

    def lanes(x):
        return lax.broadcasted_iota(jnp.int32, x.shape, 2)

    def right_of(x):
        u = pltpu.roll(x, LANE - 1, 2)
        return jnp.where(lanes(x) == LANE - 1, jnp.concatenate([u[1:], zt], 0), u)

    def left_of(x):
        u = pltpu.roll(x, 1, 2)
        return jnp.where(lanes(x) == 0, jnp.concatenate([zt, u[:-1]], 0), u)

    def dcol(x):
        return right_of(x) - left_of(x)

    avg_copy = remote(TOT, RECVA, a_send, a_recv, (1, b))
    win_copy = remote(FLUX, RECVW, w_send, w_recv, (1, nxt))

    iota = lax.broadcasted_iota(jnp.int32, (16, LANE), 0).astype(jnp.float32)
    iotas = [(iota + 16.0 * g).astype(jnp.bfloat16) for g in range(16)]
    zero = jnp.zeros((16, LANE), jnp.bfloat16)
    one = jnp.ones((16, LANE), jnp.bfloat16)

    def rows16(ref, k, *idx):
        return jnp.broadcast_to(ref[(k,) + idx], (16, LANE)).astype(jnp.bfloat16)

    def plan(base):
        loads[3].wait()
        loads[4].wait()
        for k in range(2):
            t = TG[k]
            row = lax.shift_right_logical(t, 11) - base
            cell = lax.bitwise_and(lax.shift_right_logical(t, 8), 7) * 8 + row
            inside = jnp.logical_and(row >= 0, row < 8)
            TH[k] = jnp.where(inside, cell, 255).astype(jnp.float32)
            TL[k] = lax.bitwise_and(t, 255).astype(jnp.float32)

        def build(i, carry):
            k = i // 8
            r = i % 8
            for j in range(nt):
                tl = rows16(TL, k, j, pl.ds(r, 1), slice(None))
                for g in range(16):
                    RHS[i, pl.ds(16 * g, 16), pl.ds(LANE * j, LANE)] = jnp.where(tl == iotas[g], one, zero)
            return carry

        lax.fori_loop(0, 16, build, 0)

    def scatter(avg_ref):
        for k in range(2):
            w = WT[k].astype(jnp.float32) * 0.25
            for ch in range(3):
                v = avg_ref[ch] * w
                hi = v.astype(jnp.bfloat16).astype(jnp.float32)
                VALS[k, 2 * ch] = hi
                VALS[k, 2 * ch + 1] = v - hi
        ACC[...] = jnp.zeros_like(ACC)

        def body(i, carry):
            k = i // 8
            r = i % 8
            total = None
            for jj in range(nt // 2):
                halves = []
                for j in (2 * jj, 2 * jj + 1):
                    th = rows16(TH, k, j, pl.ds(r, 1), slice(None))
                    masks = [th == iotas[g] for g in range(4)]
                    parts = []
                    for m in range(6):
                        v = rows16(VALS, k, m, j, pl.ds(r, 1), slice(None))
                        parts += [jnp.where(masks[g], v, zero) for g in range(4)]
                    halves.append(jnp.concatenate(parts, 0))
                lhs = jnp.concatenate(halves, 1)
                rhs = RHS[i, :, pl.ds(2 * LANE * jj, 2 * LANE)]
                part = lax.dot_general(lhs, rhs, (((1,), (1,)), ((), ())), preferred_element_type=jnp.float32)
                total = part if total is None else total + part
            ACC[...] += total
            return carry

        lax.fori_loop(0, 16, body, 0)
        for ch in range(3):
            for cb in range(nt // 2):
                for h in range(2):
                    FLUX[ch, 2 * cb + h] = (
                        ACC[pl.ds((2 * ch) * 64 + 8 * cb, 8), pl.ds(LANE * h, LANE)]
                        + ACC[pl.ds((2 * ch + 1) * 64 + 8 * cb, 8), pl.ds(LANE * h, LANE)]
                    )

    barrier_count = 2 + has_up.astype(jnp.int32) + has_down.astype(jnp.int32)

    out_state = pltpu.make_async_copy(Q.at[0, :, :, pl.ds(OWN, 8), :], state_out, out_sem.at[0])
    out_total = pltpu.make_async_copy(TOT, coupled_out, out_sem.at[1])
    out_flux = pltpu.make_async_copy(FLUX, coupled_out, out_sem.at[1])

    @pl.when(is_ice)
    def ice():
        for c in ice_loads:
            c.start()
        for c in range(3):
            loads[c].wait()
        cov = COV[...].astype(jnp.float32)
        inv = cov / (4.0 * F[0] + 1.0)
        T[0, :, pl.ds(OWN, 8), :] = F[1] * cov * (1.0 / 3.0)
        T[1, :, pl.ds(OWN, 8), :] = inv
        for x in range(2):
            T[2 + x, :, pl.ds(OWN, 8), :] = inv * (F[2 + x] + CUR[x, :, pl.ds(OWN, 8), :])
        pl.semaphore_wait(barrier, barrier_count)
        for c in range(CHAINS):
            both(lambda d: ice_first(d, c), "start")
            both(lambda d: ice_static_copy(d, c), "start")
        TC[...] = zeros(CHAINS, 3, ct)
        for c in ice_loads:
            c.wait()
        plan(8)

        def stress(c, q, ss):
            def vel(f, s, o):
                return S[c, q, f, :, pl.ds(s + o, 8), :]

            across_y = [dcol(vel(1, s, 0)) for s in ss]
            across_x = [dcol(vel(0, s, 0)) for s in ss]
            for i, s in enumerate(ss):
                a = vel(0, s, 1) - vel(0, s, -1)
                sh = across_x[i] + (vel(1, s, 1) - vel(1, s, -1))
                dd = a + across_y[i]
                tt = a - across_y[i]
                p = T[0, pl.ds(step_t * c, ct), pl.ds(s, 8), :]
                w = p * lax.rsqrt(4.0 * (dd * dd) + (tt * tt + sh * sh) + 0.16)
                third = 2.0 / 3.0
                S[c, q, 2, :, pl.ds(s, 8), :] = third * S[c, q, 2, :, pl.ds(s, 8), :] + (2.0 * (w * dd) - p)
                S[c, q, 3, :, pl.ds(s, 8), :] = third * S[c, q, 3, :, pl.ds(s, 8), :] + 0.5 * (w * tt)
                S[c, q, 4, :, pl.ds(s, 8), :] = third * S[c, q, 4, :, pl.ds(s, 8), :] + 0.25 * (w * sh)

        def velocity(c, q, ss, to):
            def at(f, s, o):
                return S[c, q, f, :, pl.ds(s + o, 8), :]

            def static(f, s):
                return T[f, pl.ds(step_t * c, ct), pl.ds(s, 8), :]

            d12 = [dcol(at(4, s, 0)) for s in ss]
            d22 = [dcol(at(2, s, 0) - at(3, s, 0)) for s in ss]
            for i, s in enumerate(ss):
                fx = 0.25 * ((at(2, s, 1) + at(3, s, 1)) - (at(2, s, -1) + at(3, s, -1))) + 0.5 * d12[i]
                fy = 0.5 * (at(4, s, 1) - at(4, s, -1)) + 0.25 * d22[i]
                vx, vy = at(0, s, 0), at(1, s, 0)
                ca, cb = static(4, s), static(1, s)
                S[c, to, 0, :, pl.ds(s, 8), :] = ca * (vx + 0.1 * vy) + cb * fx + static(2, s)
                S[c, to, 1, :, pl.ds(s, 8), :] = ca * (vy - 0.1 * vx) + cb * fy + static(3, s)

        def add_total(c, q):
            vx, vy = S[c, q, 0, :, pl.ds(OWN, 8), :], S[c, q, 1, :, pl.ds(OWN, 8), :]
            TC[c, 0] += vx
            TC[c, 1] += vy
            TC[c, 2] += jnp.sqrt(1.0 + vx * vx + vy * vy)

        def turn(i, carry):
            p = i // CHAINS
            c = i % CHAINS
            q = lax.rem(p, 2)
            o = 1 - q
            both(lambda d: ice_copy(d, c, q), "recv")

            @pl.when(i < CHAINS)
            def _():
                for x in range(CHAINS):
                    @pl.when(c == x)
                    def _():
                        both(lambda d: ice_static_copy(d, x), "recv")

                for lo in (0, 8, 16):
                    inv = T[1, pl.ds(step_t * c, ct), pl.ds(lo, 8), :]
                    T[4, pl.ds(step_t * c, ct), pl.ds(lo, 8), :] = jnp.where(inv > 0.0, 1.0 - inv, 0.0)

            both(lambda d: ice_copy(d, c, q), "sent")

            @pl.when(jnp.logical_and(c == CHAINS - 1, p < 2))
            def _():
                pl.semaphore_signal(gate, inc=1, device_id=(1, b), device_id_type=MESH)

            for t, (ss, vs) in enumerate((((1, 9, 17), (2, 10, 18)), ((3, 11, 19), (4, 12)),
                                          ((5, 13), (6, 14)), ((7, 15), (8,)))):
                stress(c, q, ss)
                velocity(c, q, vs, o if t == 3 else q)
                if t == 3:
                    for f in (2, 3, 4):
                        S[c, o, f, :, pl.ds(OWN, 8), :] = S[c, q, f, :, pl.ds(OWN, 8), :]
                    @pl.when(p < 3)
                    def _():
                        both(lambda d: ice_copy(d, c, o), "start")
                add_total(c, o if t == 3 else q)
            return carry

        lax.fori_loop(0, 4 * CHAINS, turn, 0)
        for c in range(CHAINS):
            both(lambda d: ice_static_copy(d, c), "sent")

        def merge(pick, put):
            for c in range(CHAINS):
                v = pick(c)
                put(slice(step_t * c + 1, step_t * c + ct - 1), v[..., 1:-1, :, :])
                if c == 0:
                    put(slice(0, 1), v[..., :1, :, :])
                else:
                    edge = v[..., :1, :, :]
                    left = lax.broadcasted_iota(jnp.int32, edge.shape, edge.ndim - 1) < LANE // 2
                    put(slice(step_t * c, step_t * c + 1), jnp.where(left, before, edge))
                before = v[..., ct - 1 :, :, :]
            put(slice(step_t * CHAINS, step_t * CHAINS + 1), before)

        for x in range(3):
            def put_total(tiles, v):
                cov = COV[tiles].astype(jnp.float32)
                if x < 2:
                    TOT[x, tiles] = v * (1.0 / 16.0) - cov * CUR[x, tiles, pl.ds(OWN, 8), :]
                else:
                    TOT[x, tiles] = v * (cov * F[4, tiles] * (1.0 / 16.0))

            merge(lambda c: TC[c, x], put_total)
        avg_copy.start()
        out_total.start()
        for f in range(5):
            def put_state(tiles, v):
                Q[0, f, tiles, pl.ds(OWN, 8), :] = v

            merge(lambda c: S[c, 0, f, :, pl.ds(OWN, 8), :], put_state)
        out_state.start()
        scatter(TOT)
        win_copy.start()
        avg_copy.wait_send()
        out_state.wait()
        out_total.wait()
        win_copy.wait_send()

    @pl.when(jnp.logical_not(is_ice))
    def ocean():
        ocean_load.start()
        pl.semaphore_wait(barrier, barrier_count)
        plan(0)
        W[:, :, pl.ds(0, 8), :] = zeros(5, nt)
        W[:, :, pl.ds(24, 8), :] = zeros(5, nt)
        for c in range(3):
            loads[c].wait()
        ocean_load.wait()
        pl.semaphore_wait(gate, 1)
        both(lambda d: ocean_copy(d, 0, init), "start")
        both(ocean_static_copy, "start")
        both(ocean_static_copy, "recv")

        def level(src, dst, l, s, flow):
            px, nx, py, ny = flow
            q = src[l, :, pl.ds(s, 8), :]
            lft, rgt = left_of(q), right_of(q)
            ch = (px * (q - src[l, :, pl.ds(s - 1, 8), :]) + nx * (src[l, :, pl.ds(s + 1, 8), :] - q)
                  + py * (q - lft) + ny * (rgt - q))
            dst[l, :, pl.ds(s, 8), :] = q - (0.2 * LEVELS[l]) * ch

        def step(src, dst, starts):
            for s in starts:
                cx, cy = CUR[0, :, pl.ds(s, 8), :], CUR[1, :, pl.ds(s, 8), :]
                flow = (jnp.maximum(cx, 0.0), jnp.minimum(cx, 0.0), jnp.maximum(cy, 0.0), jnp.minimum(cy, 0.0))
                for l in range(5):
                    level(src, dst, l, s, flow)

        def phase(p, carry):
            q = lax.rem(p, 2)
            o = 1 - q

            both(lambda d: ocean_copy(d, q), "recv")
            both(lambda d: ocean_copy(d, q), "sent")
            bufs = (Q.at[q], W)
            for t in range(8):
                count = 22 - 2 * t
                starts = [1 + t + 8 * g for g in range(-(-count // 8))]
                step(bufs[t % 2], Q.at[o] if t == 7 else bufs[(t + 1) % 2], starts)

            @pl.when(p < 1)
            def _():
                pl.semaphore_wait(gate, 1)
                both(lambda d: ocean_copy(d, o), "start")

            return carry

        lax.fori_loop(0, 2, phase, 0)
        both(ocean_static_copy, "sent")
        avg_copy.wait_recv()
        scatter(RECVA)
        win_copy.wait_recv()
        for ch in range(3):
            FLUX[ch] = FLUX[ch] + RECVW[ch]
        Q[0, 0, :, pl.ds(OWN, 8), :] = Q[0, 0, :, pl.ds(OWN, 8), :] - 0.5 * FLUX[2]
        out_state.start()
        out_flux.start()
        out_state.wait()
        out_flux.wait()


def to_tiles(x):
    lead, cols = x.shape[:-2], x.shape[-1]
    y = x.reshape(lead + (8, cols // LANE, LANE))
    return jnp.swapaxes(y, -3, -2)


def from_tiles(y):
    x = jnp.swapaxes(y, -3, -2)
    return x.reshape(x.shape[:-2] + (x.shape[-2] * LANE,))


def body(n, initial, ice_forcing, ocean_current, ice_cover, targets, weights):
    cols = initial.shape[-1]
    nt = cols // LANE
    f32 = jnp.float32
    own_t = (nt, 8, LANE)
    ext_t = (nt, RB, LANE)
    ct = (nt - 1) // CHAINS + 1
    args = [to_tiles(x) for x in (initial[0], ice_forcing, ocean_current, ice_cover, targets, weights)]
    dma = pltpu.SemaphoreType.DMA
    state, coupled = pl.pallas_call(
        functools.partial(kernel, n, nt),
        out_shape=(jax.ShapeDtypeStruct((5,) + own_t, f32), jax.ShapeDtypeStruct((3,) + own_t, f32)),
        in_specs=[pl.BlockSpec(memory_space=pl.ANY)] * 6,
        out_specs=(pl.BlockSpec(memory_space=pl.ANY),) * 2,
        scratch_shapes=[
            pltpu.VMEM((CHAINS, 2, 5, ct, RB, LANE), f32),
            pltpu.VMEM((2, 5) + ext_t, f32),
            pltpu.VMEM((5,) + ext_t, f32),
            pltpu.VMEM((5,) + ext_t, f32),
            pltpu.VMEM((5,) + own_t, f32),
            pltpu.VMEM((2,) + ext_t, f32),
            pltpu.VMEM(own_t, jnp.int32),
            pltpu.VMEM((2,) + own_t, jnp.int32),
            pltpu.VMEM((2,) + own_t, jnp.int32),
            pltpu.VMEM((CHAINS, 3, ct, 8, LANE), f32),
            pltpu.VMEM((3,) + own_t, f32),
            pltpu.VMEM((2, 6) + own_t, f32),
            pltpu.VMEM((2,) + own_t, f32),
            pltpu.VMEM((2,) + own_t, f32),
            pltpu.VMEM((16, 256, cols), jnp.bfloat16),
            pltpu.VMEM((384, 256), f32),
            pltpu.VMEM((3,) + own_t, f32),
            pltpu.VMEM((3,) + own_t, f32),
            pltpu.VMEM((3,) + own_t, f32),
            dma((5 + CHAINS,)), dma((2, CHAINS, 2)), dma((2, CHAINS, 2)), dma((2, 2)), dma((2, 2)),
            dma((2, CHAINS)), dma((2, CHAINS)),
            dma, dma, dma, dma, dma((2,)), pltpu.SemaphoreType.REGULAR,
        ],
        compiler_params=pltpu.CompilerParams(collective_id=0, has_side_effects=True),
    )(*args)
    return from_tiles(state)[None], from_tiles(coupled)[None]


def solution(mesh):
    placed = (
        P("comp", None, "blk", None),
        P(None, "blk", None),
        P(None, "blk", None),
        P("blk", None),
        P(None, "blk", None),
        P(None, "blk", None),
    )
    return jax.shard_map(
        functools.partial(body, mesh.shape["blk"]),
        mesh=mesh,
        in_specs=placed,
        out_specs=(P("comp", None, "blk", None), P("comp", None, "blk", None)),
        check_vma=False,
    )
```

time: 90.5 us -> 77.1 us (0.85)
  Pallas kernels: 87.3 us -> 73.8 us
    pallas_call x1, Pallas kernels: 87.3 us -> 73.8 us  [body(): pl.pallas_call(functools.partial(kernel, n, nt), out_shape=(jax.ShapeDtyp...]
where the time goes in v2:
time: 77.1 us; the launch traced here: 76.9 us
  Pallas kernels  73.8 us (96%)
  local copies, waits for them, and re-layouts  2.44 us (3%)
    pallas_call x1, Pallas kernels, body(): pl.pallas_call(functools.partial(kernel, n, nt), out_shape=(jax.ShapeDtyp...  73.8 us
    unnamed x4, local copies, waits for them, and re-layouts  2.44 us

profile of v2, /device:TPU:65, one launch (start us, length us, event | category | flops | bytes accessed | tf_op | source)
XLA Modules:
  0.0 76.9 jit_solution(16981009033888188088)
XLA Ops:
  0.6 73.8 %shard_map.77 = (f32[5,16,8,128]{3,2,1,0:T(8,128)}, f32[3,16,8,128]{3,2,1,0:T(8,128)}) custom-call(f32[5,16,8,128]{3,2,1,0:T(8,128)} %bitcast.25, f32[5,16,8,128]{3,2,1,0:T(8,128)} %bitcast.26, f32[2,16,8,128]{3,2,1,0:T(8,128)} %bitcast.28, s32[16,8,128]{2,1,0:T(8,128)} %bitcast.31, s32[2,16,8,128]{3,2,1,0:T(8,128)} %bitcast.29, s32[2,16,8,128]{3,2,1,0:T(8,128)} %bitcast.30), custom_call_target="tpu_custom_call" | custom-call | tf_op jit(solution)/shard_map/pallas_call | solution.py:456
  74.5 0.0 copy-start
  74.5 1.8 %copy.10 = f32[1,5,8,2048]{3,2,1,0:T(8,128)} copy(f32[1,5,8,2048]{3,2,1,0:T(8,128)} %bitcast.24) | data formatting | bytes 655360
  76.2 0.0 copy-done
  76.2 0.7 copy.11
Async XLA Ops:
  74.5 1.8 %copy-start = (f32[3,16,8,128]{3,2,1,0:T(8,128)S(1)}, f32[3,16,8,128]{3,2,1,0:T(8,128)}, u32[]{:S(2)}) copy-start(f32[3,16,8,128]{3,2,1,0:T(8,128)} %get-tuple-element.5) | copy-start | bytes 589828

commit v3 on v2

--- a/solution.py
+++ b/solution.py
@@ -17,7 +17,7 @@
 
 def kernel(n, nt, init, forcing, current, cover, targets, weights, state_out, coupled_out,
            S, Q, W, T, F, CUR, COV, TG, WT, TC, TOT, VALS, TH, TL, RHS, ACC, FLUX, RECVW, RECVA,
-           load_sem, ice_send, ice_recv, q_send, q_recv, st_send, st_recv, a_send, a_recv, w_send, w_recv,
+           load_sem, ice_send, ice_recv, st_send, st_recv, a_send, a_recv, w_send, w_recv,
            out_sem, gate):
     comp = lax.axis_index("comp")
     b = lax.axis_index("blk")
@@ -60,7 +60,6 @@
         pltpu.make_async_copy(init.at[:, pl.ds(step_t * c, ct)], S.at[c, 0, :, :, pl.ds(OWN, 8), :], load_sem.at[5 + c])
         for c in range(CHAINS)
     ]
-    ocean_load = pltpu.make_async_copy(init, Q.at[0, :, :, pl.ds(OWN, 8), :], load_sem.at[5])
     for c in loads:
         c.start()
 
@@ -68,18 +67,11 @@
         return jnp.zeros(shape + (8, LANE), jnp.float32)
 
     def zero_rows(lo):
-        @pl.when(is_ice)
-        def _():
-            for c in range(CHAINS):
-                for q in range(2):
-                    S[c, q, :, :, pl.ds(lo, 8), :] = zeros(5, ct)
-            T[:, :, pl.ds(lo, 8), :] = zeros(5, nt)
-
-        @pl.when(jnp.logical_not(is_ice))
-        def _():
+        for c in range(CHAINS):
             for q in range(2):
-                Q[q, :, :, pl.ds(lo, 8), :] = zeros(5, nt)
-            CUR[:, :, pl.ds(lo, 8), :] = zeros(2, nt)
+                S[c, q, :, :, pl.ds(lo, 8), :] = zeros(5, ct)
+        T[:, :, pl.ds(lo, 8), :] = zeros(5, nt)
+        CUR[:, :, pl.ds(lo, 8), :] = zeros(2, nt)
 
     @pl.when(jnp.logical_not(has_up))
     def _():
@@ -112,11 +104,6 @@
         tiles = pl.ds(t0, step_t * c + ct - t0)
         return remote(T.at[pl.ds(0, 4), tiles, pl.ds(OWN, 8), :], T.at[pl.ds(0, 4), tiles, pl.ds(lo, 8), :],
                       st_send.at[d, c], st_recv.at[d, c], dev)
-
-    def ocean_copy(d, q, src=None):
-        lo, dev = beside(d)
-        src = Q.at[q, :, :, pl.ds(OWN, 8), :] if src is None else src
-        return remote(src, Q.at[q, :, :, pl.ds(lo, 8), :], q_send.at[d, q], q_recv.at[d, q], dev)
 
     def ocean_static_copy(d):
         lo, dev = beside(d)
@@ -178,8 +165,8 @@
             r = i % 8
             for j in range(nt):
                 tl = rows16(TL, k, j, pl.ds(r, 1), slice(None))
-                for g in range(16):
-                    RHS[i, pl.ds(16 * g, 16), pl.ds(LANE * j, LANE)] = jnp.where(tl == iotas[g], one, zero)
+                hot = [jnp.where(tl == iotas[g], one, zero) for g in range(16)]
+                RHS[i, :, pl.ds(LANE * j, LANE)] = jnp.concatenate(hot, 0)
             return carry
 
         lax.fori_loop(0, 16, build, 0)
@@ -194,28 +181,27 @@
                 VALS[k, 2 * ch + 1] = v - hi
         ACC[...] = jnp.zeros_like(ACC)
 
-        def body(i, carry):
-            k = i // 8
-            r = i % 8
+        def body(r, carry):
             total = None
-            for jj in range(nt // 2):
-                halves = []
-                for j in (2 * jj, 2 * jj + 1):
-                    th = rows16(TH, k, j, pl.ds(r, 1), slice(None))
-                    masks = [th == iotas[g] for g in range(4)]
-                    parts = []
-                    for m in range(6):
-                        v = rows16(VALS, k, m, j, pl.ds(r, 1), slice(None))
-                        parts += [jnp.where(masks[g], v, zero) for g in range(4)]
-                    halves.append(jnp.concatenate(parts, 0))
-                lhs = jnp.concatenate(halves, 1)
-                rhs = RHS[i, :, pl.ds(2 * LANE * jj, 2 * LANE)]
-                part = lax.dot_general(lhs, rhs, (((1,), (1,)), ((), ())), preferred_element_type=jnp.float32)
-                total = part if total is None else total + part
+            for k in range(2):
+                for jj in range(nt // 2):
+                    halves = []
+                    for j in (2 * jj, 2 * jj + 1):
+                        th = rows16(TH, k, j, pl.ds(r, 1), slice(None))
+                        masks = [th == iotas[g] for g in range(4)]
+                        parts = []
+                        for m in range(6):
+                            v = rows16(VALS, k, m, j, pl.ds(r, 1), slice(None))
+                            parts += [jnp.where(masks[g], v, zero) for g in range(4)]
+                        halves.append(jnp.concatenate(parts, 0))
+                    lhs = jnp.concatenate(halves, 1)
+                    rhs = RHS[8 * k + r, :, pl.ds(2 * LANE * jj, 2 * LANE)]
+                    part = lax.dot_general(lhs, rhs, (((1,), (1,)), ((), ())), preferred_element_type=jnp.float32)
+                    total = part if total is None else total + part
             ACC[...] += total
             return carry
 
-        lax.fori_loop(0, 16, body, 0)
+        lax.fori_loop(0, 8, body, 0)
         for ch in range(3):
             for cb in range(nt // 2):
                 for h in range(2):
@@ -226,9 +212,29 @@
 
     barrier_count = 2 + has_up.astype(jnp.int32) + has_down.astype(jnp.int32)
 
-    out_state = pltpu.make_async_copy(Q.at[0, :, :, pl.ds(OWN, 8), :], state_out, out_sem.at[0])
+    out_state = pltpu.make_async_copy(Q, state_out, out_sem.at[0])
     out_total = pltpu.make_async_copy(TOT, coupled_out, out_sem.at[1])
     out_flux = pltpu.make_async_copy(FLUX, coupled_out, out_sem.at[1])
+
+    def merge(pick, put):
+        for c in range(CHAINS):
+            v = pick(c)
+            put(slice(step_t * c + 1, step_t * c + ct - 1), v[..., 1:-1, :, :])
+            if c == 0:
+                put(slice(0, 1), v[..., :1, :, :])
+            else:
+                edge = v[..., :1, :, :]
+                left = lax.broadcasted_iota(jnp.int32, edge.shape, edge.ndim - 1) < LANE // 2
+                put(slice(step_t * c, step_t * c + 1), jnp.where(left, before, edge))
+            before = v[..., ct - 1 :, :, :]
+        put(slice(step_t * CHAINS, step_t * CHAINS + 1), before)
+
+    def merge_state():
+        for f in range(5):
+            def put_state(tiles, v):
+                Q[f, tiles] = v
+
+            merge(lambda c: S[c, 0, f, :, pl.ds(OWN, 8), :], put_state)
 
     @pl.when(is_ice)
     def ice():
@@ -312,7 +318,7 @@
 
             both(lambda d: ice_copy(d, c, q), "sent")
 
-            @pl.when(jnp.logical_and(c == CHAINS - 1, p < 2))
+            @pl.when(i == 2)
             def _():
                 pl.semaphore_signal(gate, inc=1, device_id=(1, b), device_id_type=MESH)
 
@@ -333,19 +339,6 @@
         for c in range(CHAINS):
             both(lambda d: ice_static_copy(d, c), "sent")
 
-        def merge(pick, put):
-            for c in range(CHAINS):
-                v = pick(c)
-                put(slice(step_t * c + 1, step_t * c + ct - 1), v[..., 1:-1, :, :])
-                if c == 0:
-                    put(slice(0, 1), v[..., :1, :, :])
-                else:
-                    edge = v[..., :1, :, :]
-                    left = lax.broadcasted_iota(jnp.int32, edge.shape, edge.ndim - 1) < LANE // 2
-                    put(slice(step_t * c, step_t * c + 1), jnp.where(left, before, edge))
-                before = v[..., ct - 1 :, :, :]
-            put(slice(step_t * CHAINS, step_t * CHAINS + 1), before)
-
         for x in range(3):
             def put_total(tiles, v):
                 cov = COV[tiles].astype(jnp.float32)
@@ -357,11 +350,7 @@
             merge(lambda c: TC[c, x], put_total)
         avg_copy.start()
         out_total.start()
-        for f in range(5):
-            def put_state(tiles, v):
-                Q[0, f, tiles, pl.ds(OWN, 8), :] = v
-
-            merge(lambda c: S[c, 0, f, :, pl.ds(OWN, 8), :], put_state)
+        merge_state()
         out_state.start()
         scatter(TOT)
         win_copy.start()
@@ -372,61 +361,71 @@
 
     @pl.when(jnp.logical_not(is_ice))
     def ocean():
-        ocean_load.start()
+        for c in ice_loads:
+            c.start()
         pl.semaphore_wait(barrier, barrier_count)
         plan(0)
-        W[:, :, pl.ds(0, 8), :] = zeros(5, nt)
-        W[:, :, pl.ds(24, 8), :] = zeros(5, nt)
+        W[:, :, pl.ds(0, 8), :] = zeros(5, ct)
+        W[:, :, pl.ds(24, 8), :] = zeros(5, ct)
         for c in range(3):
             loads[c].wait()
-        ocean_load.wait()
+        for c in ice_loads:
+            c.wait()
         pl.semaphore_wait(gate, 1)
-        both(lambda d: ocean_copy(d, 0, init), "start")
         both(ocean_static_copy, "start")
+        for c in range(CHAINS):
+            both(lambda d: ice_first(d, c), "start")
         both(ocean_static_copy, "recv")
 
-        def level(src, dst, l, s, flow):
+        def get(c, slot, l, s):
+            return W[l, :, pl.ds(s, 8), :] if slot is None else S[c, slot, l, :, pl.ds(s, 8), :]
+
+        def level(c, src, dst, l, s, flow):
             px, nx, py, ny = flow
-            q = src[l, :, pl.ds(s, 8), :]
+            q = get(c, src, l, s)
             lft, rgt = left_of(q), right_of(q)
-            ch = (px * (q - src[l, :, pl.ds(s - 1, 8), :]) + nx * (src[l, :, pl.ds(s + 1, 8), :] - q)
-                  + py * (q - lft) + ny * (rgt - q))
-            dst[l, :, pl.ds(s, 8), :] = q - (0.2 * LEVELS[l]) * ch
-
-        def step(src, dst, starts):
+            ch = px * (q - get(c, src, l, s - 1)) + nx * (get(c, src, l, s + 1) - q) + py * (q - lft) + ny * (rgt - q)
+            new = q - (0.2 * LEVELS[l]) * ch
+            if dst is None:
+                W[l, :, pl.ds(s, 8), :] = new
+            else:
+                S[c, dst, l, :, pl.ds(s, 8), :] = new
+
+        def step(c, src, dst, starts):
             for s in starts:
-                cx, cy = CUR[0, :, pl.ds(s, 8), :], CUR[1, :, pl.ds(s, 8), :]
+                cx, cy = (CUR[x, pl.ds(step_t * c, ct), pl.ds(s, 8), :] for x in range(2))
                 flow = (jnp.maximum(cx, 0.0), jnp.minimum(cx, 0.0), jnp.maximum(cy, 0.0), jnp.minimum(cy, 0.0))
                 for l in range(5):
-                    level(src, dst, l, s, flow)
-
-        def phase(p, carry):
+                    level(c, src, dst, l, s, flow)
+
+        def turn(i, carry):
+            p = i // CHAINS
+            c = i % CHAINS
             q = lax.rem(p, 2)
             o = 1 - q
-
-            both(lambda d: ocean_copy(d, q), "recv")
-            both(lambda d: ocean_copy(d, q), "sent")
-            bufs = (Q.at[q], W)
+            both(lambda d: ice_copy(d, c, q), "recv")
+            both(lambda d: ice_copy(d, c, q), "sent")
+            slots = (q, None)
             for t in range(8):
                 count = 22 - 2 * t
                 starts = [1 + t + 8 * g for g in range(-(-count // 8))]
-                step(bufs[t % 2], Q.at[o] if t == 7 else bufs[(t + 1) % 2], starts)
+                step(c, slots[t % 2], o if t == 7 else slots[(t + 1) % 2], starts)
 
             @pl.when(p < 1)
             def _():
-                pl.semaphore_wait(gate, 1)
-                both(lambda d: ocean_copy(d, o), "start")
+                both(lambda d: ice_copy(d, c, o), "start")
 
             return carry
 
-        lax.fori_loop(0, 2, phase, 0)
+        lax.fori_loop(0, 2 * CHAINS, turn, 0)
+        merge_state()
         both(ocean_static_copy, "sent")
         avg_copy.wait_recv()
         scatter(RECVA)
         win_copy.wait_recv()
         for ch in range(3):
             FLUX[ch] = FLUX[ch] + RECVW[ch]
-        Q[0, 0, :, pl.ds(OWN, 8), :] = Q[0, 0, :, pl.ds(OWN, 8), :] - 0.5 * FLUX[2]
+        Q[0] = Q[0] - 0.5 * FLUX[2]
         out_state.start()
         out_flux.start()
         out_state.wait()
@@ -460,8 +459,8 @@
         out_specs=(pl.BlockSpec(memory_space=pl.ANY),) * 2,
         scratch_shapes=[
             pltpu.VMEM((CHAINS, 2, 5, ct, RB, LANE), f32),
-            pltpu.VMEM((2, 5) + ext_t, f32),
-            pltpu.VMEM((5,) + ext_t, f32),
+            pltpu.VMEM((5,) + own_t, f32),
+            pltpu.VMEM((5, ct, RB, LANE), f32),
             pltpu.VMEM((5,) + ext_t, f32),
             pltpu.VMEM((5,) + own_t, f32),
             pltpu.VMEM((2,) + ext_t, f32),
@@ -478,7 +477,7 @@
             pltpu.VMEM((3,) + own_t, f32),
             pltpu.VMEM((3,) + own_t, f32),
             pltpu.VMEM((3,) + own_t, f32),
-            dma((5 + CHAINS,)), dma((2, CHAINS, 2)), dma((2, CHAINS, 2)), dma((2, 2)), dma((2, 2)),
+            dma((5 + CHAINS,)), dma((2, CHAINS, 2)), dma((2, CHAINS, 2)),
             dma((2, CHAINS)), dma((2, CHAINS)),
             dma, dma, dma, dma, dma((2,)), pltpu.SemaphoreType.REGULAR,
         ],

time: 77.1 us -> 76.6 us (level)
  no operation moved by 1% of the time
where the time goes in v3:
time: 76.6 us; the launch traced here: 76.4 us
  Pallas kernels  73.3 us (96%)
  local copies, waits for them, and re-layouts  2.44 us (3%)
    pallas_call x1, Pallas kernels, body(): pl.pallas_call(functools.partial(kernel, n, nt), out_shape=(jax.ShapeDtyp...  73.3 us
    unnamed x4, local copies, waits for them, and re-layouts  2.44 us

profile of v3, /device:TPU:65, one launch (start us, length us, event | category | flops | bytes accessed | tf_op | source)
XLA Modules:
  0.0 76.4 jit_solution(17040930484494847424)
XLA Ops:
  0.6 73.3 %shard_map.77 = (f32[5,16,8,128]{3,2,1,0:T(8,128)}, f32[3,16,8,128]{3,2,1,0:T(8,128)}) custom-call(f32[5,16,8,128]{3,2,1,0:T(8,128)} %bitcast.25, f32[5,16,8,128]{3,2,1,0:T(8,128)} %bitcast.26, f32[2,16,8,128]{3,2,1,0:T(8,128)} %bitcast.28, s32[16,8,128]{2,1,0:T(8,128)} %bitcast.31, s32[2,16,8,128]{3,2,1,0:T(8,128)} %bitcast.29, s32[2,16,8,128]{3,2,1,0:T(8,128)} %bitcast.30), custom_call_target="tpu_custom_call" | custom-call | tf_op jit(solution)/shard_map/pallas_call | solution.py:455
  74.0 0.0 copy-start
  74.0 1.8 %copy.10 = f32[1,5,8,2048]{3,2,1,0:T(8,128)} copy(f32[1,5,8,2048]{3,2,1,0:T(8,128)} %bitcast.24) | data formatting | bytes 655360
  75.7 0.0 copy-done
  75.7 0.7 copy.11
Async XLA Ops:
  74.0 1.8 %copy-start = (f32[3,16,8,128]{3,2,1,0:T(8,128)S(1)}, f32[3,16,8,128]{3,2,1,0:T(8,128)}, u32[]{:S(2)}) copy-start(f32[3,16,8,128]{3,2,1,0:T(8,128)} %get-tuple-element.5) | copy-start | bytes 589828
